TPU v7x, 32 devices: a whole 2x2x4 slice. The times are simulated.
32 devices in a mesh: inl: 4 (over z), xln: 8 (over y, x, core).
Axes of the slice: x: 2, y: 2, z: 4, core: 2. Of those that a mesh axis runs over, the one named last changes fastest.
Arguments:
- noisy: float32 [128, 256, 512], P('inl', 'xln'), may hold values from -6 to 6
- bound: float32 [128, 256, 512], P('inl', 'xln'), may hold values from 0.05 to 0.5
Outputs:
- denoised: float32 [128, 256, 512], P('inl', 'xln')
- dual: float32 [3, 128, 256, 512], P(None, 'inl', 'xln')
- norms: float32 [2, 2], replicated
All inputs are finite; a program needn't handle non-finite values.
Results may differ from a plain program's by a relative error of at most 0.0001.
Values sent between devices are 32-bit elements; how exact they have to be, the bound alone decides.
A program may use at most 64 MiB of HBM per device.

v0:
```python
import jax
import jax.numpy as jnp
from jax import lax
from jax.sharding import PartitionSpec as P

ITERS = 2
SIGMA = 0.28
TAU = 0.28


def passed_along(value, axis, steps):
    count = lax.axis_size(axis)
    first, last = (max(0, -steps), min(count, count - steps))
    return lax.ppermute(value, axis, [(source, source + steps) for source in range(first, last)])


def depth_forward(field):
    return jnp.concatenate(
        [field[:, :, 1:] - field[:, :, :-1], jnp.zeros_like(field[:, :, :1])], axis=2
    )


def depth_backward(field):
    return field - jnp.concatenate([jnp.zeros_like(field[:, :, :1]), field[:, :, :-1]], axis=2)


def finish(sums_list):
    return jnp.sqrt(lax.psum(jnp.stack(sums_list), ("inl", "xln")))


def record(primal_sum, dual_sum, sums_list):
    sums_list.append(jnp.stack([primal_sum, dual_sum]))


def per_device(noisy, bound):
    sums_list = []
    inl_flag = (lax.axis_index("inl") < lax.axis_size("inl") - 1).astype(jnp.float32)
    xln_flag = (lax.axis_index("xln") < lax.axis_size("xln") - 1).astype(jnp.float32)
    primal = noisy
    smooth = noisy
    dual_i = jnp.zeros_like(noisy)
    dual_x = jnp.zeros_like(noisy)
    dual_z = jnp.zeros_like(noisy)
    for step in range(ITERS):
        next_i = passed_along(smooth[0:1], "inl", -1)
        next_x = passed_along(smooth[:, 0:1], "xln", -1)
        grad_i = jnp.concatenate(
            [smooth[1:] - smooth[:-1], (next_i - smooth[-1:]) * inl_flag], axis=0
        )
        grad_x = jnp.concatenate(
            [smooth[:, 1:] - smooth[:, :-1], (next_x - smooth[:, -1:]) * xln_flag], axis=1
        )
        fresh_i = jnp.clip(dual_i + SIGMA * grad_i, -bound, bound)
        fresh_x = jnp.clip(dual_x + SIGMA * grad_x, -bound, bound)
        fresh_z = jnp.clip(dual_z + SIGMA * depth_forward(smooth), -bound, bound)
        prev_i = passed_along(fresh_i[-1:], "inl", 1)
        prev_x = passed_along(fresh_x[:, -1:], "xln", 1)
        diverge = fresh_i - jnp.concatenate([prev_i, fresh_i[:-1]], axis=0)
        diverge = diverge + (fresh_x - jnp.concatenate([prev_x, fresh_x[:, :-1]], axis=1))
        diverge = diverge + depth_backward(fresh_z)
        updated = (primal + TAU * diverge + TAU * noisy) / (1.0 + TAU)
        primal_sum = jnp.sum((updated - primal) ** 2)
        dual_sum = (
            jnp.sum((fresh_i - dual_i) ** 2)
            + jnp.sum((fresh_x - dual_x) ** 2)
            + jnp.sum((fresh_z - dual_z) ** 2)
        )
        record(primal_sum, dual_sum, sums_list)
        smooth = 2.0 * updated - primal
        primal = updated
        dual_i, dual_x, dual_z = (fresh_i, fresh_x, fresh_z)
    norms = finish(sums_list)
    return (primal, jnp.stack([dual_i, dual_x, dual_z]), norms)


def solution(mesh):
    in_specs = (P("inl", "xln", None), P("inl", "xln", None))
    out_specs = (P("inl", "xln", None), P(None, "inl", "xln", None), P())
    return jax.shard_map(
        per_device, mesh=mesh, in_specs=in_specs, out_specs=out_specs, check_vma=False
    )
```

profile of v0, /device:TPU:0, one launch (start us, length us, event | category | flops | bytes accessed | tf_op | source)
XLA Modules:
  0.0 110.8 jit_solution(10471086511929388984)
XLA Ops:
  0.6 0.8 slice.92
  1.5 1.3 %collective-permute-start = (f32[1,32,512]{2,1,0:T(8,128)S(1)}, f32[1,32,512]{2,1,0:T(8,128)S(1)}, u32[]{:S(2)}, u32[]{:S(2)}) collective-permute-start(f32[1,32,512]{2,1,0:T(8,128)S(1)} %slice.92), channel_id=1, source_target_pairs={{8,0},{16,8},{24,16},{9,1},{17,9},{25,17},{10,2},{18,10},{26,18},{... | collective-permute-start | bytes 196616 | tf_op jit(solution)/shard_map/ppermute | solution.py:14
  2.8 1.1 slice.98
  3.9 1.4 %collective-permute-start.2 = (f32[32,1,512]{2,1,0:T(1,128)S(1)}, f32[32,1,512]{2,1,0:T(1,128)S(1)}, u32[]{:S(2)}, u32[]{:S(2)}) collective-permute-start(f32[32,1,512]{2,1,0:T(1,128)S(1)} %slice.98), channel_id=1, source_target_pairs={{1,0},{2,1},{3,2},{4,3},{5,4},{6,5},{7,6},{9,8},{10,9},{11,10},{12... | collective-permute-start | bytes 196616 | tf_op jit(solution)/shard_map/ppermute | solution.py:14
  5.3 4.1 %slice_subtract_fusion.3 = f32[32,31,512]{2,1,0:T(8,128)} fusion(f32[32,32,512]{2,1,0:T(8,128)} %param.2), kind=kLoop, calls=%fused_computation.44 | loop fusion | flops 507904 | bytes 6094848 | tf_op jit(solution)/shard_map/sub | solution.py:51
  9.4 2.0 %slice_subtract_fusion.2 = f32[32,32,511]{2,1,0:T(8,128)} fusion(f32[32,32,512]{2,1,0:T(8,128)S(1)} %copy-done), kind=kLoop, calls=%fused_computation.43 | loop fusion | flops 523264 | bytes 6279168 | tf_op jit(solution)/shard_map/sub | solution.py:19
  11.3 1.7 %slice_subtract_fusion.5 = f32[31,32,512]{2,1,0:T(8,128)} fusion(f32[32,32,512]{2,1,0:T(8,128)S(1)} %copy-done), kind=kLoop, calls=%fused_computation.46 | loop fusion | flops 507904 | bytes 6094848 | tf_op jit(solution)/shard_map/sub | solution.py:48
  13.1 4.5 %fusion.1 = (f32[32,32,512]{2,1,0:T(8,128)S(1)}, f32[32,32,512]{2,1,0:T(8,128)S(1)}, f32[32,32,512]{2,1,0:T(8,128)S(1)}) fusion(f32[32,32,512]{2,1,0:T(8,128)} %param.3, f32[1,32,512]{2,1,0:T(8,128)S(1)} %subtract_multiply_fusion.1, f32[31,32,512]{2,1,0:T(8,128)} %slice_subtract_fusion.5, f32[32,32,511]{2,1,0:T(8,128)} %slice_subtract_fusion.2, ...), kind=kLoop, calls=%fused_computation.5 | loop fusion | flops 6291456 | bytes 14675968 | tf_op jit(solution)/shard_map/jit(clip)/min | solution.py:53
  17.7 3.0 %collective-permute-start.3 = (f32[32,1,512]{2,1,0:T(1,128)S(1)}, f32[32,1,512]{2,1,0:T(1,128)S(1)}, u32[]{:S(2)}, u32[]{:S(2)}) collective-permute-start(f32[32,1,512]{2,1,0:T(1,128)S(1)} %slice.122), channel_id=1, source_target_pairs={{0,1},{1,2},{2,3},{3,4},{4,5},{5,6},{6,7},{8,9},{9,10},{10,11},{11... | collective-permute-start | bytes 196616 | tf_op jit(solution)/shard_map/ppermute | solution.py:14
  20.8 5.6 %collective-permute-start.1 = (f32[1,32,512]{2,1,0:T(8,128)S(1)}, f32[1,32,512]{2,1,0:T(8,128)S(1)}, u32[]{:S(2)}, u32[]{:S(2)}) collective-permute-start(f32[1,32,512]{2,1,0:T(8,128)S(1)} %slice.120), channel_id=1, source_target_pairs={{0,8},{8,16},{16,24},{1,9},{9,17},{17,25},{2,10},{10,18},{18,26},{... | collective-permute-start | bytes 196616 | tf_op jit(solution)/shard_map/ppermute | solution.py:14
  26.6 1.6 %collective-permute-done.1 = f32[1,32,512]{2,1,0:T(8,128)S(1)} collective-permute-done((f32[1,32,512]{2,1,0:T(8,128)S(1)}, f32[1,32,512]{2,1,0:T(8,128)S(1)}, u32[]{:S(2)}, u32[]{:S(2)}) %collective-permute-start.1) | collective-permute-done | bytes 65568 | tf_op jit(solution)/shard_map/ppermute | solution.py:14
  28.3 3.5 %multiply_subtract_fusion = (f32[32,32,512]{2,1,0:T(8,128)S(1)}, f32[32,32,512]{2,1,0:T(8,128)}) fusion(f32[32,32,512]{2,1,0:T(8,128)S(1)} %copy-done, f32[32,32,512]{2,1,0:T(8,128)S(1)} %get-tuple-element.24, f32[32,32,511]{2,1,0:T(8,128)S(1)} %bitcast.18, f32[32,32,512]{2,1,0:T(8,128)S(1)} %get-tuple-element.25, f32[32,31,512]{2,1,0:T(8,128)S(1)} %bitcast.15, ...), kind=kLoop, calls=%fused_computation.41 | loop fusion | flops 6815744 | bytes 18870272 | tf_op jit(solution)/shard_map/sub | solution.py:69
  32.1 0.6 slice_subtract_fusion
  32.7 1.4 %collective-permute-start.4 = (f32[1,32,512]{2,1,0:T(8,128)S(1)}, f32[1,32,512]{2,1,0:T(8,128)S(1)}, u32[]{:S(2)}, u32[]{:S(2)}) collective-permute-start(f32[1,32,512]{2,1,0:T(8,128)S(1)} %slice.127), channel_id=1, source_target_pairs={{8,0},{16,8},{24,16},{9,1},{17,9},{25,17},{10,2},{18,10},{26,18},{... | collective-permute-start | bytes 196616 | tf_op jit(solution)/shard_map/ppermute | solution.py:14
  34.4 1.3 %collective-permute-start.6 = (f32[32,1,512]{2,1,0:T(1,128)S(1)}, f32[32,1,512]{2,1,0:T(1,128)S(1)}, u32[]{:S(2)}, u32[]{:S(2)}) collective-permute-start(f32[32,1,512]{2,1,0:T(1,128)S(1)} %slice.133), channel_id=1, source_target_pairs={{1,0},{2,1},{3,2},{4,3},{5,4},{6,5},{7,6},{9,8},{10,9},{11,10},{12... | collective-permute-start | bytes 196616 | tf_op jit(solution)/shard_map/ppermute | solution.py:14
  35.7 4.2 %collective-permute-done.4 = f32[1,32,512]{2,1,0:T(8,128)S(1)} collective-permute-done((f32[1,32,512]{2,1,0:T(8,128)S(1)}, f32[1,32,512]{2,1,0:T(8,128)S(1)}, u32[]{:S(2)}, u32[]{:S(2)}) %collective-permute-start.4) | collective-permute-done | bytes 65568 | tf_op jit(solution)/shard_map/ppermute | solution.py:14
  40.0 3.8 %multiply_reduce_fusion.6 = (f32[]{:T(128)}, f32[]{:T(128)}, f32[32,32,512]{2,1,0:T(8,128)S(1)}, f32[]{:T(128)}, f32[32,32,512]{2,1,0:T(8,128)}, /*index=5*/f32[...) fusion(f32[32,32,512]{2,1,0:T(8,128)S(1)} %get-tuple-element.23, f32[32,32,512]{2,1,0:T(8,128)S(1)} %copy-done.6, ...), kind=kLoop, calls=%fused_computation.38 | loop fusion | flops 15728634 | bytes 20967448 | tf_op jit(solution)/shard_map/reduce_sum | solution.py:64
  43.9 2.7 %collective-permute-start.7 = (f32[32,1,512]{2,1,0:T(1,128)S(1)}, f32[32,1,512]{2,1,0:T(1,128)S(1)}, u32[]{:S(2)}, u32[]{:S(2)}) collective-permute-start(f32[32,1,512]{2,1,0:T(1,128)S(1)} %slice.135), channel_id=1, source_target_pairs={{0,1},{1,2},{2,3},{3,4},{4,5},{5,6},{6,7},{8,9},{9,10},{10,11},{11... | collective-permute-start | bytes 196616 | tf_op jit(solution)/shard_map/ppermute | solution.py:14
  46.6 4.7 %collective-permute-start.5 = (f32[1,32,512]{2,1,0:T(8,128)S(1)}, f32[1,32,512]{2,1,0:T(8,128)S(1)}, u32[]{:S(2)}, u32[]{:S(2)}) collective-permute-start(f32[1,32,512]{2,1,0:T(8,128)S(1)} %slice.129), channel_id=1, source_target_pairs={{0,8},{8,16},{16,24},{1,9},{9,17},{17,25},{2,10},{10,18},{18,26},{... | collective-permute-start | bytes 196616 | tf_op jit(solution)/shard_map/ppermute | solution.py:14
  51.4 1.5 %slice.130 = f32[31,32,512]{2,1,0:T(8,128)} slice(f32[32,32,512]{2,1,0:T(8,128)S(1)} %get-tuple-element.14), slice={[0:31], [0:32], [0:512]} | slice | bytes 4063232 | tf_op jit(solution)/shard_map/slice | solution.py:58
  56.7 8.3 %multiply_reduce_fusion.7 = (f32[]{:T(128)}, f32[]{:T(128)}, f32[32,32,512]{2,1,0:T(8,128)}) fusion(f32[32,32,512]{2,1,0:T(8,128)S(1)} %copy-done, f32[32,32,512]{2,1,0:T(8,128)} %get-tuple-element.16, f32[32,32,512]{2,1,0:T(8,128)} %get-tuple-element.18, f32[32,32,511]{2,1,0:T(8,128)} %bitcast.19, f32[32,32,512]{2,1,0:T(8,128)} %copy-done.1, ...), kind=kLoop, calls=%fused_computation.39 | loop fusion | flops 9961470 | bytes 18870280 | tf_op jit(solution)/shard_map/reduce_sum | solution.py:62
  65.0 1.4 %maximum_bitcast_fusion = (f32[1,2]{1,0:T(1,128)S(1)}, f32[1,2]{1,0:T(1,128)S(1)}) fusion(f32[1]{0:T(128)} %bitcast.4, f32[1]{0:T(128)} %bitcast.3, f32[1]{0:T(128)} %bitcast.7, f32[1]{0:T(128)} %bitcast.6), kind=kLoop, calls=%fused_computation.54 | loop fusion | flops 4 | bytes 32 | tf_op jit(solution)/shard_map/stack | solution.py:28
  66.4 3.4 %pad_maximum_fusion = f32[3,32,32,512]{3,2,1,0:T(8,128)} fusion(f32[1,32,32,512]{3,2,1,0:T(8,128)S(1)} %bitcast.20, f32[1,32,32,512]{3,2,1,0:T(8,128)S(1)} %bitcast.17, f32[1,32,32,512]{3,2,1,0:T(8,128)S(1)} %bitcast.21), kind=kLoop, calls=%fused_computation | loop fusion | flops 3145728 | bytes 12582912 | tf_op jit(solution)/shard_map/stack | solution.py:73
  69.8 40.5 %psum.7 = f32[2,2]{1,0:T(2,128)S(1)} all-reduce(f32[2,2]{1,0:T(2,128)S(1)} %pad_maximum_fusion.1), channel_id=1, replica_groups=mesh['inl'=4,'xln'=8] {'inl','xln'}, use_global_device_ids=true, to_apply=%region_8.9 | all-reduce | flops 4 | bytes 32 | tf_op jit(solution)/shard_map/psum | solution.py:28
  (35 shorter events, 1.8 us)
Async XLA Ops:
  1.5 11.5 %collective-permute-start = (f32[1,32,512]{2,1,0:T(8,128)S(1)}, f32[1,32,512]{2,1,0:T(8,128)S(1)}, u32[]{:S(2)}, u32[]{:S(2)}) collective-permute-start(f32[1,32,512]{2,1,0:T(8,128)S(1)} %slice.92), channel_id=1, source_target_pairs={{8,0},{16,8},{24,16},{9,1},{17,9},{25,17},{10,2},{18,10},{26,18},{... | collective-permute-start | bytes 196616 | tf_op jit(solution)/shard_map/ppermute | solution.py:14
  3.8 5.5 %copy-start = (f32[32,32,512]{2,1,0:T(8,128)S(1)}, f32[32,32,512]{2,1,0:T(8,128)}, u32[]{:S(2)}) copy-start(f32[32,32,512]{2,1,0:T(8,128)} %param.2) | copy-start | bytes 6291460
  3.9 9.2 %collective-permute-start.2 = (f32[32,1,512]{2,1,0:T(1,128)S(1)}, f32[32,1,512]{2,1,0:T(1,128)S(1)}, u32[]{:S(2)}, u32[]{:S(2)}) collective-permute-start(f32[32,1,512]{2,1,0:T(1,128)S(1)} %slice.98), channel_id=1, source_target_pairs={{1,0},{2,1},{3,2},{4,3},{5,4},{6,5},{7,6},{9,8},{10,9},{11,10},{12... | collective-permute-start | bytes 196616 | tf_op jit(solution)/shard_map/ppermute | solution.py:14
  17.7 8.9 %collective-permute-start.3 = (f32[32,1,512]{2,1,0:T(1,128)S(1)}, f32[32,1,512]{2,1,0:T(1,128)S(1)}, u32[]{:S(2)}, u32[]{:S(2)}) collective-permute-start(f32[32,1,512]{2,1,0:T(1,128)S(1)} %slice.122), channel_id=1, source_target_pairs={{0,1},{1,2},{2,3},{3,4},{4,5},{5,6},{6,7},{8,9},{9,10},{10,11},{11... | collective-permute-start | bytes 196616 | tf_op jit(solution)/shard_map/ppermute | solution.py:14
  20.8 7.5 %collective-permute-start.1 = (f32[1,32,512]{2,1,0:T(8,128)S(1)}, f32[1,32,512]{2,1,0:T(8,128)S(1)}, u32[]{:S(2)}, u32[]{:S(2)}) collective-permute-start(f32[1,32,512]{2,1,0:T(8,128)S(1)} %slice.120), channel_id=1, source_target_pairs={{0,8},{8,16},{16,24},{1,9},{9,17},{17,25},{2,10},{10,18},{18,26},{... | collective-permute-start | bytes 196616 | tf_op jit(solution)/shard_map/ppermute | solution.py:14
  32.7 7.3 %copy-start.6 = (f32[32,32,512]{2,1,0:T(8,128)S(1)}, f32[32,32,512]{2,1,0:T(8,128)}, u32[]{:S(2)}) copy-start(f32[32,32,512]{2,1,0:T(8,128)} %param.3) | copy-start | bytes 6291460
  32.7 7.2 %collective-permute-start.4 = (f32[1,32,512]{2,1,0:T(8,128)S(1)}, f32[1,32,512]{2,1,0:T(8,128)S(1)}, u32[]{:S(2)}, u32[]{:S(2)}) collective-permute-start(f32[1,32,512]{2,1,0:T(8,128)S(1)} %slice.127), channel_id=1, source_target_pairs={{8,0},{16,8},{24,16},{9,1},{17,9},{25,17},{10,2},{18,10},{26,18},{... | collective-permute-start | bytes 196616 | tf_op jit(solution)/shard_map/ppermute | solution.py:14
  34.4 5.5 %collective-permute-start.6 = (f32[32,1,512]{2,1,0:T(1,128)S(1)}, f32[32,1,512]{2,1,0:T(1,128)S(1)}, u32[]{:S(2)}, u32[]{:S(2)}) collective-permute-start(f32[32,1,512]{2,1,0:T(1,128)S(1)} %slice.133), channel_id=1, source_target_pairs={{1,0},{2,1},{3,2},{4,3},{5,4},{6,5},{7,6},{9,8},{10,9},{11,10},{12... | collective-permute-start | bytes 196616 | tf_op jit(solution)/shard_map/ppermute | solution.py:14
  43.8 9.1 %copy-start.1 = (f32[32,32,512]{2,1,0:T(8,128)}, f32[32,32,512]{2,1,0:T(8,128)S(1)}, u32[]{:S(2)}) copy-start(f32[32,32,512]{2,1,0:T(8,128)S(1)} %get-tuple-element.21) | copy-start | bytes 6291460
  43.8 9.1 %copy-start.4 = (f32[32,32,512]{2,1,0:T(8,128)}, f32[32,32,512]{2,1,0:T(8,128)S(1)}, u32[]{:S(2)}) copy-start(f32[32,32,512]{2,1,0:T(8,128)S(1)} %get-tuple-element.14) | copy-start | bytes 6291460
  43.9 12.7 %collective-permute-start.7 = (f32[32,1,512]{2,1,0:T(1,128)S(1)}, f32[32,1,512]{2,1,0:T(1,128)S(1)}, u32[]{:S(2)}, u32[]{:S(2)}) collective-permute-start(f32[32,1,512]{2,1,0:T(1,128)S(1)} %slice.135), channel_id=1, source_target_pairs={{0,1},{1,2},{2,3},{3,4},{4,5},{5,6},{6,7},{8,9},{9,10},{10,11},{11... | collective-permute-start | bytes 196616 | tf_op jit(solution)/shard_map/ppermute | solution.py:14
  46.6 10.0 %collective-permute-start.5 = (f32[1,32,512]{2,1,0:T(8,128)S(1)}, f32[1,32,512]{2,1,0:T(8,128)S(1)}, u32[]{:S(2)}, u32[]{:S(2)}) collective-permute-start(f32[1,32,512]{2,1,0:T(8,128)S(1)} %slice.129), channel_id=1, source_target_pairs={{0,8},{8,16},{16,24},{1,9},{9,17},{17,25},{2,10},{10,18},{18,26},{... | collective-permute-start | bytes 196616 | tf_op jit(solution)/shard_map/ppermute | solution.py:14
  56.7 9.7 %copy-start.2 = (f32[32,32,512]{2,1,0:T(8,128)S(1)}, f32[32,32,512]{2,1,0:T(8,128)}, u32[]{:S(2)}) copy-start(f32[32,32,512]{2,1,0:T(8,128)} %copy-done.1) | copy-start | bytes 6291460
  56.7 9.7 %copy-start.3 = (f32[32,32,512]{2,1,0:T(8,128)S(1)}, f32[32,32,512]{2,1,0:T(8,128)}, u32[]{:S(2)}) copy-start(f32[32,32,512]{2,1,0:T(8,128)} %get-tuple-element.18) | copy-start | bytes 6291460
  56.7 9.7 %copy-start.5 = (f32[32,32,512]{2,1,0:T(8,128)S(1)}, f32[32,32,512]{2,1,0:T(8,128)}, u32[]{:S(2)}) copy-start(f32[32,32,512]{2,1,0:T(8,128)} %copy-done.4) | copy-start | bytes 6291460
where the time goes:
time: 111 us
  blocking collectives  40.5 us (36%)
  other arithmetic  33.9 us (31%)
  starting transfers between devices  21.5 us (19%)
  waiting for transfers between devices  5.79 us (5%)
  between operations  4.65 us (4%)
  local copies, waits for them, and re-layouts  4.5 us (4%)
    psum x1, blocking collectives, finish(): return jnp.sqrt(lax.psum(jnp.stack(sums_list), ('inl', 'xln')))  40.5 us
    ppermute x8, starting transfers between devices, passed_along(): lax.ppermute(value, axis, [(source, source + steps) for source in range(f...  21.5 us
    reduce_sum x1, other arithmetic, per_device(): primal_sum = jnp.sum((updated - primal) ** 2)  8.26 us
    ppermute x8, waiting for transfers between devices, passed_along(): lax.ppermute(value, axis, [(source, source + steps) for source in range(f...  5.79 us
    min x1, other arithmetic, per_device(): fresh_i = jnp.clip(dual_i + SIGMA * grad_i, -bound, bound)  4.53 us
    sub x2, other arithmetic, per_device(): smooth[:, 1:] - smooth[:, :-1]  4.4 us
    reduce_sum x1, other arithmetic, per_device(): jnp.sum((fresh_i - dual_i) ** 2) + jnp.sum((fresh_x - dual_x) ** 2)  3.83 us
    sub x1, other arithmetic, per_device(): smooth = 2.0 * updated - primal  3.47 us
  transfers between devices with their start and end apart: 8, of which 2 were waited for; matrix products, arithmetic and copies ran while one was open for 10% of the time, Pallas kernels for 0%

commit v1 on v0

--- a/solution.py
+++ b/solution.py
@@ -25,7 +25,7 @@
 
 
 def finish(sums_list):
-    return jnp.sqrt(lax.psum(jnp.stack(sums_list), ("inl", "xln")))
+    return jnp.sqrt(lax.psum(lax.psum(jnp.stack(sums_list), "xln"), "inl"))
 
 
 def record(primal_sum, dual_sum, sums_list):

time: 111 us -> 96.8 us (0.87)
  blocking collectives: 40.5 us -> 22.3 us
  other arithmetic: 33.9 us -> 37.4 us
    psum x1 -> x2, blocking collectives: 40.5 us -> 22.3 us  [finish(): return jnp.sqrt(lax.psum(lax.psum(jnp.stack(sums_list), 'xln'), 'inl'))]
    another operation x1, other arithmetic: 3.41 us -> 6.89 us  [per_device(): return (primal, jnp.stack([dual_i, dual_x, dual_z]), norms)]
  transfers between devices with their start and end apart: 8 -> 8, of which waited for: 2 -> 2; matrix products, arithmetic and copies ran while one was open for 10% -> 11% of each run, Pallas kernels for 0% -> 0%
where the time goes in v1:
time: 96.8 us; the launch traced here: 96 us
  other arithmetic  37.4 us (39%)
  blocking collectives  22.3 us (23%)
  starting transfers between devices  21.5 us (22%)
  waiting for transfers between devices  5.79 us (6%)
  between operations  4.55 us (5%)
  local copies, waits for them, and re-layouts  4.46 us (5%)
    psum x2, blocking collectives, finish(): return jnp.sqrt(lax.psum(lax.psum(jnp.stack(sums_list), 'xln'), 'inl'))  22.3 us
    ppermute x8, starting transfers between devices, passed_along(): lax.ppermute(value, axis, [(source, source + steps) for source in range(f...  21.5 us
    reduce_sum x1, other arithmetic, per_device(): primal_sum = jnp.sum((updated - primal) ** 2)  8.23 us
    another operation x1, other arithmetic, per_device(): return (primal, jnp.stack([dual_i, dual_x, dual_z]), norms)  6.89 us
    ppermute x8, waiting for transfers between devices, passed_along(): lax.ppermute(value, axis, [(source, source + steps) for source in range(f...  5.79 us
    min x1, other arithmetic, per_device(): fresh_i = jnp.clip(dual_i + SIGMA * grad_i, -bound, bound)  4.53 us
    sub x2, other arithmetic, per_device(): smooth[:, 1:] - smooth[:, :-1]  4.4 us
    reduce_sum x1, other arithmetic, per_device(): jnp.sum((fresh_i - dual_i) ** 2) + jnp.sum((fresh_x - dual_x) ** 2)  3.92 us
  transfers between devices with their start and end apart: 8, of which 2 were waited for; matrix products, arithmetic and copies ran while one was open for 11% of the time, Pallas kernels for 0%

profile of v1, /device:TPU:0, one launch (start us, length us, event | category | flops | bytes accessed | tf_op | source)
XLA Modules:
  0.0 96.0 jit_solution(15639891389835570270)
XLA Ops:
  0.6 0.8 slice.92
  1.5 1.3 %collective-permute-start = (f32[1,32,512]{2,1,0:T(8,128)S(1)}, f32[1,32,512]{2,1,0:T(8,128)S(1)}, u32[]{:S(2)}, u32[]{:S(2)}) collective-permute-start(f32[1,32,512]{2,1,0:T(8,128)S(1)} %slice.92), channel_id=1, source_target_pairs={{8,0},{16,8},{24,16},{9,1},{17,9},{25,17},{10,2},{18,10},{26,18},{... | collective-permute-start | bytes 196616 | tf_op jit(solution)/shard_map/ppermute | solution.py:14
  2.8 1.1 %slice.98 = f32[32,1,512]{2,1,0:T(1,128)S(1)} slice(f32[32,32,512]{2,1,0:T(8,128)} %param.2), slice={[0:32], [0:1], [0:512]} | slice | bytes 131072 | tf_op jit(solution)/shard_map/slice | solution.py:46
  3.9 1.4 %collective-permute-start.2 = (f32[32,1,512]{2,1,0:T(1,128)S(1)}, f32[32,1,512]{2,1,0:T(1,128)S(1)}, u32[]{:S(2)}, u32[]{:S(2)}) collective-permute-start(f32[32,1,512]{2,1,0:T(1,128)S(1)} %slice.98), channel_id=1, source_target_pairs={{1,0},{2,1},{3,2},{4,3},{5,4},{6,5},{7,6},{9,8},{10,9},{11,10},{12... | collective-permute-start | bytes 196616 | tf_op jit(solution)/shard_map/ppermute | solution.py:14
  5.3 4.1 %slice_subtract_fusion.3 = f32[32,31,512]{2,1,0:T(8,128)} fusion(f32[32,32,512]{2,1,0:T(8,128)} %param.2), kind=kLoop, calls=%fused_computation.44 | loop fusion | flops 507904 | bytes 6094848 | tf_op jit(solution)/shard_map/sub | solution.py:51
  9.4 2.0 %slice_subtract_fusion.2 = f32[32,32,511]{2,1,0:T(8,128)} fusion(f32[32,32,512]{2,1,0:T(8,128)S(1)} %copy-done), kind=kLoop, calls=%fused_computation.43 | loop fusion | flops 523264 | bytes 6279168 | tf_op jit(solution)/shard_map/sub | solution.py:19
  11.3 1.7 %slice_subtract_fusion.5 = f32[31,32,512]{2,1,0:T(8,128)} fusion(f32[32,32,512]{2,1,0:T(8,128)S(1)} %copy-done), kind=kLoop, calls=%fused_computation.46 | loop fusion | flops 507904 | bytes 6094848 | tf_op jit(solution)/shard_map/sub | solution.py:48
  13.1 4.5 %fusion.1 = (f32[32,32,512]{2,1,0:T(8,128)S(1)}, f32[32,32,512]{2,1,0:T(8,128)S(1)}, f32[32,32,512]{2,1,0:T(8,128)S(1)}) fusion(f32[32,32,512]{2,1,0:T(8,128)} %param.3, f32[1,32,512]{2,1,0:T(8,128)S(1)} %subtract_multiply_fusion.1, f32[31,32,512]{2,1,0:T(8,128)} %slice_subtract_fusion.5, f32[32,32,511]{2,1,0:T(8,128)} %slice_subtract_fusion.2, ...), kind=kLoop, calls=%fused_computation.5 | loop fusion | flops 6291456 | bytes 14675968 | tf_op jit(solution)/shard_map/jit(clip)/min | solution.py:53
  17.7 3.0 %collective-permute-start.3 = (f32[32,1,512]{2,1,0:T(1,128)S(1)}, f32[32,1,512]{2,1,0:T(1,128)S(1)}, u32[]{:S(2)}, u32[]{:S(2)}) collective-permute-start(f32[32,1,512]{2,1,0:T(1,128)S(1)} %slice.122), channel_id=1, source_target_pairs={{0,1},{1,2},{2,3},{3,4},{4,5},{5,6},{6,7},{8,9},{9,10},{10,11},{11... | collective-permute-start | bytes 196616 | tf_op jit(solution)/shard_map/ppermute | solution.py:14
  20.8 5.6 %collective-permute-start.1 = (f32[1,32,512]{2,1,0:T(8,128)S(1)}, f32[1,32,512]{2,1,0:T(8,128)S(1)}, u32[]{:S(2)}, u32[]{:S(2)}) collective-permute-start(f32[1,32,512]{2,1,0:T(8,128)S(1)} %slice.120), channel_id=1, source_target_pairs={{0,8},{8,16},{16,24},{1,9},{9,17},{17,25},{2,10},{10,18},{18,26},{... | collective-permute-start | bytes 196616 | tf_op jit(solution)/shard_map/ppermute | solution.py:14
  26.6 1.6 %collective-permute-done.1 = f32[1,32,512]{2,1,0:T(8,128)S(1)} collective-permute-done((f32[1,32,512]{2,1,0:T(8,128)S(1)}, f32[1,32,512]{2,1,0:T(8,128)S(1)}, u32[]{:S(2)}, u32[]{:S(2)}) %collective-permute-start.1) | collective-permute-done | bytes 65568 | tf_op jit(solution)/shard_map/ppermute | solution.py:14
  28.3 3.5 %multiply_subtract_fusion = (f32[32,32,512]{2,1,0:T(8,128)S(1)}, f32[32,32,512]{2,1,0:T(8,128)}) fusion(f32[32,32,512]{2,1,0:T(8,128)S(1)} %copy-done, f32[32,32,512]{2,1,0:T(8,128)S(1)} %get-tuple-element.24, f32[32,32,511]{2,1,0:T(8,128)S(1)} %bitcast.18, f32[32,32,512]{2,1,0:T(8,128)S(1)} %get-tuple-element.25, f32[32,31,512]{2,1,0:T(8,128)S(1)} %bitcast.15, ...), kind=kLoop, calls=%fused_computation.41 | loop fusion | flops 6815744 | bytes 18870272 | tf_op jit(solution)/shard_map/sub | solution.py:69
  32.7 1.4 %collective-permute-start.4 = (f32[1,32,512]{2,1,0:T(8,128)S(1)}, f32[1,32,512]{2,1,0:T(8,128)S(1)}, u32[]{:S(2)}, u32[]{:S(2)}) collective-permute-start(f32[1,32,512]{2,1,0:T(8,128)S(1)} %slice.127), channel_id=1, source_target_pairs={{8,0},{16,8},{24,16},{9,1},{17,9},{25,17},{10,2},{18,10},{26,18},{... | collective-permute-start | bytes 196616 | tf_op jit(solution)/shard_map/ppermute | solution.py:14
  34.4 1.3 %collective-permute-start.6 = (f32[32,1,512]{2,1,0:T(1,128)S(1)}, f32[32,1,512]{2,1,0:T(1,128)S(1)}, u32[]{:S(2)}, u32[]{:S(2)}) collective-permute-start(f32[32,1,512]{2,1,0:T(1,128)S(1)} %slice.133), channel_id=1, source_target_pairs={{1,0},{2,1},{3,2},{4,3},{5,4},{6,5},{7,6},{9,8},{10,9},{11,10},{12... | collective-permute-start | bytes 196616 | tf_op jit(solution)/shard_map/ppermute | solution.py:14
  35.7 4.2 %collective-permute-done.4 = f32[1,32,512]{2,1,0:T(8,128)S(1)} collective-permute-done((f32[1,32,512]{2,1,0:T(8,128)S(1)}, f32[1,32,512]{2,1,0:T(8,128)S(1)}, u32[]{:S(2)}, u32[]{:S(2)}) %collective-permute-start.4) | collective-permute-done | bytes 65568 | tf_op jit(solution)/shard_map/ppermute | solution.py:14
  40.0 3.9 %multiply_reduce_fusion.6 = (f32[]{:T(128)}, f32[]{:T(128)}, f32[32,32,512]{2,1,0:T(8,128)S(1)}, f32[]{:T(128)}, f32[32,32,512]{2,1,0:T(8,128)}, /*index=5*/f32[...) fusion(f32[32,32,512]{2,1,0:T(8,128)S(1)} %get-tuple-element.23, f32[32,32,512]{2,1,0:T(8,128)S(1)} %copy-done.3, ...), kind=kLoop, calls=%fused_computation.38 | loop fusion | flops 15728634 | bytes 20967448 | tf_op jit(solution)/shard_map/reduce_sum | solution.py:64
  44.0 2.7 %collective-permute-start.7 = (f32[32,1,512]{2,1,0:T(1,128)S(1)}, f32[32,1,512]{2,1,0:T(1,128)S(1)}, u32[]{:S(2)}, u32[]{:S(2)}) collective-permute-start(f32[32,1,512]{2,1,0:T(1,128)S(1)} %slice.135), channel_id=1, source_target_pairs={{0,1},{1,2},{2,3},{3,4},{4,5},{5,6},{6,7},{8,9},{9,10},{10,11},{11... | collective-permute-start | bytes 196616 | tf_op jit(solution)/shard_map/ppermute | solution.py:14
  46.7 4.7 %collective-permute-start.5 = (f32[1,32,512]{2,1,0:T(8,128)S(1)}, f32[1,32,512]{2,1,0:T(8,128)S(1)}, u32[]{:S(2)}, u32[]{:S(2)}) collective-permute-start(f32[1,32,512]{2,1,0:T(8,128)S(1)} %slice.129), channel_id=1, source_target_pairs={{0,8},{8,16},{16,24},{1,9},{9,17},{17,25},{2,10},{10,18},{18,26},{... | collective-permute-start | bytes 196616 | tf_op jit(solution)/shard_map/ppermute | solution.py:14
  51.4 1.5 %slice.130 = f32[31,32,512]{2,1,0:T(8,128)} slice(f32[32,32,512]{2,1,0:T(8,128)S(1)} %get-tuple-element.14), slice={[0:31], [0:32], [0:512]} | slice | bytes 4063232 | tf_op jit(solution)/shard_map/slice | solution.py:58
  56.7 8.2 %multiply_reduce_fusion.7 = (f32[]{:T(128)}, f32[]{:T(128)}, f32[32,32,512]{2,1,0:T(8,128)}) fusion(f32[32,32,512]{2,1,0:T(8,128)S(1)} %copy-done, f32[32,32,512]{2,1,0:T(8,128)} %get-tuple-element.16, f32[32,32,512]{2,1,0:T(8,128)} %get-tuple-element.18, f32[32,32,511]{2,1,0:T(8,128)} %bitcast.19, f32[32,32,512]{2,1,0:T(8,128)} %copy-done.1, ...), kind=kLoop, calls=%fused_computation.39 | loop fusion | flops 9961470 | bytes 18870280 | tf_op jit(solution)/shard_map/reduce_sum | solution.py:62
  64.9 1.3 %maximum_bitcast_fusion = (f32[1,2]{1,0:T(1,128)S(1)}, f32[1,2]{1,0:T(1,128)S(1)}) fusion(f32[1]{0:T(128)} %bitcast.4, f32[1]{0:T(128)} %bitcast.3, f32[1]{0:T(128)} %bitcast.7, f32[1]{0:T(128)} %bitcast.6), kind=kLoop, calls=%fused_computation.54 | loop fusion | flops 4 | bytes 32 | tf_op jit(solution)/shard_map/stack | solution.py:28
  66.2 11.8 %psum.14 = f32[2,2]{1,0:T(2,128)S(1)} all-reduce(f32[2,2]{1,0:T(2,128)S(1)} %pad_maximum_fusion.1), channel_id=1, replica_groups=mesh['inl'=4,'xln'=8] {'xln'}, use_global_device_ids=true, to_apply=%region_8.9 | all-reduce | flops 4 | bytes 32 | tf_op jit(solution)/shard_map/psum | solution.py:28
  78.0 6.9 %pad_maximum_fusion = f32[3,32,32,512]{3,2,1,0:T(8,128)} fusion(f32[1,32,32,512]{3,2,1,0:T(8,128)} %bitcast.20, f32[1,32,32,512]{3,2,1,0:T(8,128)} %bitcast.17, f32[1,32,32,512]{3,2,1,0:T(8,128)} %bitcast.21), kind=kLoop, calls=%fused_computation | loop fusion | flops 3145728 | bytes 12582912 | tf_op jit(solution)/shard_map/stack | solution.py:73
  84.9 10.5 %psum.15 = f32[2,2]{1,0:T(2,128)S(1)} all-reduce(f32[2,2]{1,0:T(2,128)S(1)} %psum.14), channel_id=1, replica_groups=mesh['inl'=4,'xln'=8] {'inl'}, use_global_device_ids=true, to_apply=%region_9.10 | all-reduce | flops 4 | bytes 32 | tf_op jit(solution)/shard_map/psum | solution.py:28
  (30 shorter events, 2.4 us)
Async XLA Ops:
  1.5 11.5 %collective-permute-start = (f32[1,32,512]{2,1,0:T(8,128)S(1)}, f32[1,32,512]{2,1,0:T(8,128)S(1)}, u32[]{:S(2)}, u32[]{:S(2)}) collective-permute-start(f32[1,32,512]{2,1,0:T(8,128)S(1)} %slice.92), channel_id=1, source_target_pairs={{8,0},{16,8},{24,16},{9,1},{17,9},{25,17},{10,2},{18,10},{26,18},{... | collective-permute-start | bytes 196616 | tf_op jit(solution)/shard_map/ppermute | solution.py:14
  3.8 5.5 %copy-start = (f32[32,32,512]{2,1,0:T(8,128)S(1)}, f32[32,32,512]{2,1,0:T(8,128)}, u32[]{:S(2)}) copy-start(f32[32,32,512]{2,1,0:T(8,128)} %param.2) | copy-start | bytes 6291460
  3.9 9.2 %collective-permute-start.2 = (f32[32,1,512]{2,1,0:T(1,128)S(1)}, f32[32,1,512]{2,1,0:T(1,128)S(1)}, u32[]{:S(2)}, u32[]{:S(2)}) collective-permute-start(f32[32,1,512]{2,1,0:T(1,128)S(1)} %slice.98), channel_id=1, source_target_pairs={{1,0},{2,1},{3,2},{4,3},{5,4},{6,5},{7,6},{9,8},{10,9},{11,10},{12... | collective-permute-start | bytes 196616 | tf_op jit(solution)/shard_map/ppermute | solution.py:14
  17.7 8.9 %collective-permute-start.3 = (f32[32,1,512]{2,1,0:T(1,128)S(1)}, f32[32,1,512]{2,1,0:T(1,128)S(1)}, u32[]{:S(2)}, u32[]{:S(2)}) collective-permute-start(f32[32,1,512]{2,1,0:T(1,128)S(1)} %slice.122), channel_id=1, source_target_pairs={{0,1},{1,2},{2,3},{3,4},{4,5},{5,6},{6,7},{8,9},{9,10},{10,11},{11... | collective-permute-start | bytes 196616 | tf_op jit(solution)/shard_map/ppermute | solution.py:14
  20.8 7.5 %collective-permute-start.1 = (f32[1,32,512]{2,1,0:T(8,128)S(1)}, f32[1,32,512]{2,1,0:T(8,128)S(1)}, u32[]{:S(2)}, u32[]{:S(2)}) collective-permute-start(f32[1,32,512]{2,1,0:T(8,128)S(1)} %slice.120), channel_id=1, source_target_pairs={{0,8},{8,16},{16,24},{1,9},{9,17},{17,25},{2,10},{10,18},{18,26},{... | collective-permute-start | bytes 196616 | tf_op jit(solution)/shard_map/ppermute | solution.py:14
  32.7 7.3 %copy-start.3 = (f32[32,32,512]{2,1,0:T(8,128)S(1)}, f32[32,32,512]{2,1,0:T(8,128)}, u32[]{:S(2)}) copy-start(f32[32,32,512]{2,1,0:T(8,128)} %param.3) | copy-start | bytes 6291460
  32.7 7.2 %collective-permute-start.4 = (f32[1,32,512]{2,1,0:T(8,128)S(1)}, f32[1,32,512]{2,1,0:T(8,128)S(1)}, u32[]{:S(2)}, u32[]{:S(2)}) collective-permute-start(f32[1,32,512]{2,1,0:T(8,128)S(1)} %slice.127), channel_id=1, source_target_pairs={{8,0},{16,8},{24,16},{9,1},{17,9},{25,17},{10,2},{18,10},{26,18},{... | collective-permute-start | bytes 196616 | tf_op jit(solution)/shard_map/ppermute | solution.py:14
  34.4 5.5 %collective-permute-start.6 = (f32[32,1,512]{2,1,0:T(1,128)S(1)}, f32[32,1,512]{2,1,0:T(1,128)S(1)}, u32[]{:S(2)}, u32[]{:S(2)}) collective-permute-start(f32[32,1,512]{2,1,0:T(1,128)S(1)} %slice.133), channel_id=1, source_target_pairs={{1,0},{2,1},{3,2},{4,3},{5,4},{6,5},{7,6},{9,8},{10,9},{11,10},{12... | collective-permute-start | bytes 196616 | tf_op jit(solution)/shard_map/ppermute | solution.py:14
  43.9 9.0 %copy-start.1 = (f32[32,32,512]{2,1,0:T(8,128)}, f32[32,32,512]{2,1,0:T(8,128)S(1)}, u32[]{:S(2)}) copy-start(f32[32,32,512]{2,1,0:T(8,128)S(1)} %get-tuple-element.21) | copy-start | bytes 6291460
  43.9 9.0 %copy-start.2 = (f32[32,32,512]{2,1,0:T(8,128)}, f32[32,32,512]{2,1,0:T(8,128)S(1)}, u32[]{:S(2)}) copy-start(f32[32,32,512]{2,1,0:T(8,128)S(1)} %get-tuple-element.14) | copy-start | bytes 6291460
  44.0 12.7 %collective-permute-start.7 = (f32[32,1,512]{2,1,0:T(1,128)S(1)}, f32[32,1,512]{2,1,0:T(1,128)S(1)}, u32[]{:S(2)}, u32[]{:S(2)}) collective-permute-start(f32[32,1,512]{2,1,0:T(1,128)S(1)} %slice.135), channel_id=1, source_target_pairs={{0,1},{1,2},{2,3},{3,4},{4,5},{5,6},{6,7},{8,9},{9,10},{10,11},{11... | collective-permute-start | bytes 196616 | tf_op jit(solution)/shard_map/ppermute | solution.py:14
  46.7 10.0 %collective-permute-start.5 = (f32[1,32,512]{2,1,0:T(8,128)S(1)}, f32[1,32,512]{2,1,0:T(8,128)S(1)}, u32[]{:S(2)}, u32[]{:S(2)}) collective-permute-start(f32[1,32,512]{2,1,0:T(8,128)S(1)} %slice.129), channel_id=1, source_target_pairs={{0,8},{8,16},{16,24},{1,9},{9,17},{17,25},{2,10},{10,18},{18,26},{... | collective-permute-start | bytes 196616 | tf_op jit(solution)/shard_map/ppermute | solution.py:14
